TPU v7x, 32 devices: a whole 2x2x4 slice. The times are simulated.
32 devices in a mesh: grp: 2 (over x), freq: 16 (over z, y, core).
Axes of the slice: x: 2, y: 2, z: 4, core: 2. Of those that a mesh axis runs over, the one named last changes fastest.
Arguments:
- kernel: bfloat16 [2, 256, 1024, 1024], P(None, ('grp', 'freq')), parts along dimension 1, may hold values from -0.125 to 0.125
- recorded: float32 [2, 256, 1024, 128], P(None, ('grp', 'freq')), parts along dimension 1, may hold values from -8 to 8
- onset_time: int32 [2048, 128], P(('grp', 'freq')), parts along dimension 0, may hold values from 32 to 256, as said below
Outputs:
- focusing: float32 [256, 2048, 128], P(None, ('grp', 'freq')), parts along dimension 1
There are 2 independent parts, one for each index of `grp`. A program takes and returns all parts, laid end to end along the dimension named above; each array names one. Nothing has to cross between parts.
Inputs may be any that keep to these rules, and one draw needn't show every extreme that they name: `onset_time`: onset sample of the window for each receiver and focal point.
All inputs are finite; a program needn't handle non-finite values.
Results may differ from a plain program's by a relative error of at most 0.012.
Values may be sent and summed in bfloat16 or wider, within the bound.
A program may use at most 192 MiB of HBM per device.

v0:
```python
import math

import jax
import jax.numpy as jnp
from jax import lax
from jax.sharding import PartitionSpec as P

ITERS = 2
CHUNKS = 2


def dft_table(bins_total):
    samples = jnp.arange(2 * bins_total, dtype=jnp.int32)
    bins = jnp.arange(bins_total, dtype=jnp.int32)
    phase = (bins[:, None] * samples[None, :] % (2 * bins_total)).astype(jnp.float32) * (math.pi / bins_total)
    factor = 1.0 / math.sqrt(bins_total)
    return jnp.stack([jnp.cos(phase) * factor, -jnp.sin(phase) * factor])


def square_sum(values):
    return jnp.sum(values * values)


def make_body(mesh):
    members = mesh.shape["freq"]

    def joint(*values):
        row = jnp.zeros((128,), jnp.float32)
        for place, value in enumerate(values):
            row = row.at[place].set(value)
        spread = jnp.broadcast_to(row, (members, 128))
        got = lax.all_to_all(spread, "freq", split_axis=0, concat_axis=0, tiled=True)
        total = jnp.sum(got, axis=0)
        return [total[place] for place in range(len(values))]

    def body(kernel, recorded, onset_time):
        own_bins = kernel.shape[1]
        sources = kernel.shape[2]
        receivers = kernel.shape[3]
        rec_local, focal = onset_time.shape
        bins_total = own_bins * members
        times = 2 * bins_total
        part = own_bins // CHUNKS
        rows = 2 * part
        table = dft_table(bins_total).astype(jnp.bfloat16)
        table = table.reshape(2, members, CHUNKS, part, times)
        tables = [
            table[:, :, c].transpose(1, 0, 2, 3).reshape(members * rows, times) for c in range(CHUNKS)
        ]
        steps = lax.broadcasted_iota(jnp.int32, (rec_local, times, focal), 1)
        keep_mask = (steps < onset_time[:, None, :]).astype(jnp.float32)
        real = [kernel[0, c * part:(c + 1) * part] for c in range(CHUNKS)]
        imag = [kernel[1, c * part:(c + 1) * part] for c in range(CHUNKS)]

        def exchange(block):
            return lax.all_to_all(block, "freq", split_axis=0, concat_axis=0, tiled=True)

        def image_part(c, resid):
            low = resid.astype(jnp.bfloat16)
            turned = jnp.concatenate([low[..., focal:], -low[..., :focal]], axis=-1)
            z = jnp.einsum("hvi,hvg->hig", real[c], low, preferred_element_type=jnp.float32)
            z = z + jnp.einsum("hvi,hvg->hig", imag[c], turned, preferred_element_type=jnp.float32)
            z = z.astype(jnp.bfloat16).reshape(part, members, rec_local, 2, focal)
            z = z.transpose(1, 2, 3, 0, 4).reshape(members, rec_local, rows, focal)
            return z

        def to_time(images):
            total = 0.0
            for c in range(CHUNKS):
                block = images[c].transpose(1, 0, 2, 3).reshape(rec_local, members * rows, focal)
                total = total + jnp.einsum(
                    "kt,rkq->rtq", tables[c], block, preferred_element_type=jnp.float32
                )
            return total * keep_mask

        def to_spectrum(field):
            low = field.astype(jnp.bfloat16)
            out = []
            for c in range(CHUNKS):
                spec = jnp.einsum("kt,rtq->rkq", tables[c], low, preferred_element_type=jnp.float32)
                spec = spec.astype(jnp.bfloat16).reshape(rec_local, members, rows, focal)
                out.append(exchange(spec.transpose(1, 0, 2, 3)))
            return out

        def forward_part(c, spec):
            spec = spec.reshape(receivers, 2, part, focal).transpose(2, 0, 1, 3)
            spec = spec.reshape(part, receivers, 2 * focal)
            turned = jnp.concatenate([-spec[..., focal:], spec[..., :focal]], axis=-1)
            y = jnp.einsum("hvi,hig->hvg", real[c], spec, preferred_element_type=jnp.float32)
            return y + jnp.einsum("hvi,hig->hvg", imag[c], turned, preferred_element_type=jnp.float32)

        data = []
        for c in range(CHUNKS):
            piece = recorded[:, c * part:(c + 1) * part]
            data.append(jnp.concatenate([piece[0], piece[1]], axis=-1))
        raw = to_time([exchange(image_part(c, data[c])) for c in range(CHUNKS)])
        sum_b, sum_z = joint(square_sum(recorded), square_sum(raw))
        beta = jnp.sqrt(sum_b)
        image_norm = jnp.sqrt(sum_z)
        alpha = image_norm / beta
        field, field_scale = raw, 1.0 / image_norm
        data_scale = 1.0 / beta
        phibar, rhobar = beta, alpha
        fields = [lax.optimization_barrier(raw.transpose(1, 0, 2))]
        search = [field_scale]
        estimate = [jnp.float32(0.0)]
        for iteration in range(ITERS):
            spectra = to_spectrum(field)
            fresh = []
            images = []
            data_squares = 0.0
            for c in range(CHUNKS):
                spec = spectra[c]
                if images:
                    spec, images[-1] = lax.optimization_barrier((spec, images[-1]))
                elif fresh:
                    spec, fresh[-1] = lax.optimization_barrier((spec, fresh[-1]))
                piece = forward_part(c, spec) * field_scale - (alpha * data_scale) * data[c]
                data_squares = data_squares + square_sum(piece)
                fresh.append(piece)
                if iteration + 1 < ITERS:
                    images.append(image_part(c, piece))
            last = iteration + 1 == ITERS
            if last:
                (sum_u,) = joint(data_squares)
            else:
                image = to_time([exchange(z) for z in images])
                sum_u, sum_i, cross = joint(data_squares, square_sum(image), jnp.sum(image * field))
            beta = jnp.sqrt(sum_u)
            data, data_scale = fresh, 1.0 / beta
            rho = jnp.sqrt(rhobar * rhobar + beta * beta)
            cosine = rhobar / rho
            sine = beta / rho
            phi = cosine * phibar
            phibar = sine * phibar
            estimate = [e + phi / rho * s for e, s in zip(estimate, search)]
            if last:
                break
            field = image * data_scale - (beta * field_scale) * field
            alpha = jnp.sqrt(sum_i / sum_u - 2.0 * field_scale * cross + sum_u)
            field_scale = 1.0 / alpha
            theta = sine * alpha
            rhobar = -cosine * alpha
            fields.append(lax.optimization_barrier(field.transpose(1, 0, 2)))
            search = [-(theta / rho) * s for s in search] + [field_scale]
            estimate = estimate + [jnp.float32(0.0)]
        total = 0.0
        for e, f in zip(estimate, fields):
            total = total + e * f
        return total

    return body


def solution(mesh):
    placed = (
        P(None, ("grp", "freq"), None, None),
        P(None, ("grp", "freq"), None, None),
        P(("grp", "freq"), None),
    )
    return jax.shard_map(
        make_body(mesh), mesh=mesh, in_specs=placed, out_specs=P(None, ("grp", "freq"), None), check_vma=False
    )
```

profile of v0, /device:TPU:0, one launch (start us, length us, event | category | flops | bytes accessed | tf_op | source)
XLA Modules:
  0.0 590.9 jit_solution(11007640866443702357)
XLA Ops:
  19.4 7.3 %fusion.55 = bf16[4,1024,256]{1,2,0:T(8,128)(2,1)} fusion(f32[4,256,1024]{2,1,0:T(8,128)S(1)} %fusion.24, bf16[4,1024,256]{1,2,0:T(8,128)(2,1)S(1)} %fusion.54, bf16[2,8,1024,1024]{3,2,1,0:T(8,128)(2,1)} %param.15), kind=kOutput, calls=%fused_computation.82 | convolution fusion | flops 2149580800 | bytes 16777216 | tf_op jit(solution)/shard_map/hvi,hvg->hig/dot_general | solution.py:61
  35.1 7.5 %all-to-all-start = ((bf16[16,64,8,128]{3,1,2,0:T(8,128)(2,1)}), bf16[16,64,8,128]{3,1,2,0:T(8,128)(2,1)}, u32[]{:S(2)}, u32[]{:S(2)}) async-start(bf16[16,64,8,128]{3,1,2,0:T(8,128)(2,1)} %bitcast.7), calls=%async_computation | async-start | bytes 4194304 | tf_op jit(solution)/shard_map/all_to_all | solution.py:56
  54.3 7.3 %fusion.56 = bf16[4,1024,256]{1,2,0:T(8,128)(2,1)} fusion(f32[4,256,1024]{2,1,0:T(8,128)S(1)} %fusion.8, bf16[4,1024,256]{1,2,0:T(8,128)(2,1)S(1)} %fusion.53, bf16[2,8,1024,1024]{3,2,1,0:T(8,128)(2,1)} %param.15), kind=kOutput, calls=%fused_computation.83 | convolution fusion | flops 2149580800 | bytes 16777216 | tf_op jit(solution)/shard_map/hvi,hvg->hig/dot_general | solution.py:61
  73.0 10.7 %all-to-all-done = bf16[16,64,8,128]{3,1,2,0:T(8,128)(2,1)} async-done(((bf16[16,64,8,128]{3,1,2,0:T(8,128)(2,1)}), bf16[16,64,8,128]{3,1,2,0:T(8,128)(2,1)}, u32[]{:S(2)}, u32[]{:S(2)}) %all-to-all-start) | async-done | bytes 2097184 | tf_op jit(solution)/shard_map/all_to_all | solution.py:56
  83.6 11.5 %all-to-all-start.1 = ((bf16[16,64,8,128]{3,1,2,0:T(8,128)(2,1)}), bf16[16,64,8,128]{3,1,2,0:T(8,128)(2,1)}, u32[]{:S(2)}, u32[]{:S(2)}) async-start(bf16[16,64,8,128]{3,1,2,0:T(8,128)(2,1)} %bitcast.228), calls=%async_computation.1 | async-start | bytes 4194304 | tf_op jit(solution)/shard_map/all_to_all | solution.py:56
  102.7 8.1 %fusion.87 = f32[64,128,256]{2,1,0:T(8,128)} fusion(bf16[128,256,1]{1,0,2:T(8,128)(2,1)S(1)} %reshape.347, bf16[64,128,128]{2,0,1:T(8,128)(2,1)} %bitcast.9), kind=kOutput, calls=%fused_computation.114 | convolution fusion | flops 536870912 | bytes 10551296 | tf_op jit(solution)/shard_map/kt,rkq->rtq/dot_general | solution.py:71
  110.8 25.3 %all-to-all-done.1 = bf16[16,64,8,128]{3,1,2,0:T(8,128)(2,1)} async-done(((bf16[16,64,8,128]{3,1,2,0:T(8,128)(2,1)}), bf16[16,64,8,128]{3,1,2,0:T(8,128)(2,1)}, u32[]{:S(2)}, u32[]{:S(2)}) %all-to-all-start.1) | async-done | bytes 2097184 | tf_op jit(solution)/shard_map/all_to_all | solution.py:56
  136.1 8.3 %multiply_reduce_fusion.2 = (f32[]{:T(128)}, f32[64,128,256]{2,1,0:T(8,128)}) fusion(s32[64,128]{1,0:T(8,128)S(1)} %copy-done.10, f32[64,128,256]{2,1,0:T(8,128)} %fusion.87, bf16[128,256,1]{1,0,2:T(8,128)(2,1)S(1)} %reshape.348, bf16[64,128,128]{2,0,1:T(8,128)(2,1)} %bitcast.20), kind=kOutput, calls=%fused_computation.43 | convolution fusion | flops 547356672 | bytes 18972676 | tf_op jit(solution)/shard_map/kt,rkq->rtq/dot_general | solution.py:71
  145.7 11.2 %all-to-all-start.2 = ((f32[16,1,128]{2,1,0:T(1,128)}), f32[16,1,128]{2,1,0:T(1,128)S(1)}, u32[]{:S(2)}, u32[]{:S(2)}) async-start(f32[16,1,128]{2,1,0:T(1,128)} %broadcast_in_dim.12), calls=%async_computation.2 | async-start | bytes 16384 | tf_op jit(solution)/shard_map/all_to_all | solution.py:32
  179.4 31.7 %all-to-all-done.3 = bf16[16,64,8,128]{3,1,2,0:T(8,128)(2,1)} async-done(((bf16[16,64,8,128]{3,1,2,0:T(8,128)(2,1)}), bf16[16,64,8,128]{3,1,2,0:T(8,128)(2,1)}, u32[]{:S(2)}, u32[]{:S(2)}) %all-to-all-start.3) | async-done | bytes 2097184 | tf_op jit(solution)/shard_map/all_to_all | solution.py:56
  211.1 11.7 %all-to-all-start.4 = ((bf16[16,64,8,128]{3,1,2,0:T(8,128)(2,1)}), bf16[16,64,8,128]{3,1,2,0:T(8,128)(2,1)}, u32[]{:S(2)}, u32[]{:S(2)}) async-start(bf16[16,64,8,128]{3,1,2,0:T(8,128)(2,1)} %bitcast.226), calls=%async_computation.4 | async-start | bytes 4194304 | tf_op jit(solution)/shard_map/all_to_all | solution.py:56
  231.6 7.9 %fusion.22 = f32[4,256,1024]{2,1,0:T(8,128)} fusion(bf16[2,8,1024,1024]{3,2,1,0:T(8,128)(2,1)} %param.15, bf16[4,1024,128]{1,2,0:T(8,128)(2,1)S(1)} %get-tuple-element.106, bf16[4,1024,128]{1,2,0:T(8,128)(2,1)S(1)} %get-tuple-element.105), kind=kOutput, calls=%fused_computation.26 | convolution fusion | flops 2151677952 | bytes 14680064 | tf_op jit(solution)/shard_map/hvi,hig->hvg/dot_general | solution.py:90
  239.5 11.2 %multiply_reduce_fusion.6 = (f32[]{:T(128)}, bf16[4,1024,256]{1,2,0:T(8,128)(2,1)}, f32[4,1024,256]{1,2,0:T(8,128)}) fusion(f32[4,1024,128]{1,2,0:T(8,128)S(1)} %bitcast.225, f32[4,1024,128]{1,2,0:T(8,128)S(1)} %bitcast.223, f32[]{:T(128)S(6)} %mul.306, f32[]{:T(128)S(6)} %div.38, f32[4,256,1024]{2,1,0:T(8,128)} %fusion.22, ...), kind=kOutput, calls=%fused_computation.75 | convolution fusion | flops 2155872256 | bytes 25165836 | tf_op jit(solution)/shard_map/hvi,hig->hvg/dot_general | solution.py:89
  257.3 7.3 %fusion.57 = bf16[4,1024,256]{1,2,0:T(8,128)(2,1)} fusion(f32[4,256,1024]{2,1,0:T(8,128)S(1)} %fusion.20, bf16[4,1024,256]{1,2,0:T(8,128)(2,1)S(1)} %copy-done.9, bf16[2,8,1024,1024]{3,2,1,0:T(8,128)(2,1)} %param.15), kind=kOutput, calls=%fused_computation.84 | convolution fusion | flops 2149580800 | bytes 16777216 | tf_op jit(solution)/shard_map/hvi,hvg->hig/dot_general | solution.py:61
  292.3 8.2 %fusion.6 = f32[4,256,1024]{2,1,0:T(8,128)} fusion(bf16[2,8,1024,1024]{3,2,1,0:T(8,128)(2,1)} %param.15, bf16[4,1024,128]{1,2,0:T(8,128)(2,1)} %get-tuple-element.102, bf16[4,1024,128]{1,2,0:T(8,128)(2,1)S(1)} %get-tuple-element.101), kind=kOutput, calls=%fused_computation.10 | convolution fusion | flops 2151677952 | bytes 14680064 | tf_op jit(solution)/shard_map/hvi,hig->hvg/dot_general | solution.py:90
  300.5 10.5 %multiply_reduce_fusion.5 = (f32[]{:T(128)}, bf16[4,1024,256]{1,2,0:T(8,128)(2,1)S(1)}, f32[4,1024,256]{1,2,0:T(8,128)}) fusion(f32[4,1024,128]{1,2,0:T(8,128)S(1)} %bitcast.221, f32[4,1024,128]{1,2,0:T(8,128)S(1)} %bitcast.219, f32[]{:T(128)S(6)} %mul.306, f32[]{:T(128)S(6)} %div.38, f32[4,256,1024]{2,1,0:T(8,128)} %fusion.6, ...), kind=kOutput, calls=%fused_computation.73 | convolution fusion | flops 2155872256 | bytes 25165836 | tf_op jit(solution)/shard_map/hvi,hig->hvg/dot_general | solution.py:89
  316.0 7.3 %fusion.58 = bf16[4,1024,256]{1,2,0:T(8,128)(2,1)} fusion(f32[4,256,1024]{2,1,0:T(8,128)S(1)} %fusion.4, bf16[4,1024,256]{1,2,0:T(8,128)(2,1)S(1)} %get-tuple-element.92, bf16[2,8,1024,1024]{3,2,1,0:T(8,128)(2,1)} %param.15), kind=kOutput, calls=%fused_computation.85 | convolution fusion | flops 2149580800 | bytes 16777216 | tf_op jit(solution)/shard_map/hvi,hvg->hig/dot_general | solution.py:61
  333.2 11.4 %all-to-all-start.6 = ((bf16[16,64,8,128]{3,1,2,0:T(8,128)(2,1)}), bf16[16,64,8,128]{3,1,2,0:T(8,128)(2,1)S(1)}, u32[]{:S(2)}, u32[]{:S(2)}) async-start(bf16[16,64,8,128]{3,1,2,0:T(8,128)(2,1)} %bitcast.50), calls=%async_computation.6 | async-start | bytes 4194304 | tf_op jit(solution)/shard_map/all_to_all | solution.py:56
  345.9 7.9 %fusion.84 = f32[64,128,256]{2,1,0:T(8,128)} fusion(bf16[128,256,1]{1,0,2:T(8,128)(2,1)S(1)} %reshape.347, bf16[64,128,128]{2,0,1:T(8,128)(2,1)} %bitcast.47), kind=kOutput, calls=%fused_computation.111 | convolution fusion | flops 536870912 | bytes 10551296 | tf_op jit(solution)/shard_map/kt,rkq->rtq/dot_general | solution.py:71
  353.9 31.8 %all-to-all-done.6 = bf16[16,64,8,128]{3,1,2,0:T(8,128)(2,1)S(1)} async-done(((bf16[16,64,8,128]{3,1,2,0:T(8,128)(2,1)}), bf16[16,64,8,128]{3,1,2,0:T(8,128)(2,1)S(1)}, u32[]{:S(2)}, u32[]{:S(2)}) %all-to-all-start.6) | async-done | bytes 2097184 | tf_op jit(solution)/shard_map/all_to_all | solution.py:56
  385.6 12.6 %multiply_reduce_fusion = (f32[]{:T(128)}, f32[]{:T(128)}, f32[64,128,256]{2,1,0:T(8,128)}) fusion(f32[64,128,256]{2,1,0:T(8,128)} %get-tuple-element.121, s32[64,128]{1,0:T(8,128)S(1)} %copy-done.10, f32[64,128,256]{2,1,0:T(8,128)} %fusion.84, bf16[128,256,1]{1,0,2:T(8,128)(2,1)S(1)} %reshape.348, bf16[64,128,128]{2,0,1:T(8,128)(2,1)S(1)} %bitcast.247), kind=kOutput, calls=%fused_computation.41 | convolution fusion | flops 553648128 | bytes 27361288 | tf_op jit(solution)/shard_map/kt,rkq->rtq/dot_general | solution.py:71
  399.5 17.4 %all_to_all.58 = f32[16,1,128]{2,1,0:T(1,128)S(1)} all-to-all(f32[16,1,128]{2,1,0:T(1,128)S(1)} %broadcast_in_dim.13), channel_id=1, replica_groups=mesh['grp'=2,'freq'=16] {'freq'}, dimensions={0} | all-to-all | bytes 16384 | tf_op jit(solution)/shard_map/all_to_all | solution.py:32
  418.3 7.0 %subtract_convert_fusion = bf16[64,256,128]{1,2,0:T(8,128)(2,1)S(1)} fusion(f32[64,128,256]{2,1,0:T(8,128)} %get-tuple-element.124, f32[64,128,256]{2,1,0:T(8,128)} %get-tuple-element.121, f32[]{:T(128)S(6)} %mul.325, f32[]{:T(128)S(6)} %div.43, s32[64,128]{1,0:T(8,128)S(1)} %copy-done.10), kind=kLoop, calls=%fused_computation.40 | loop fusion | flops 14680064 | bytes 21004296 | tf_op jit(solution)/shard_map/convert_element_type | solution.py:77
  439.7 34.5 %all-to-all-done.8 = bf16[16,64,8,128]{3,1,2,0:T(8,128)(2,1)S(1)} async-done(((bf16[16,64,8,128]{3,1,2,0:T(8,128)(2,1)}), bf16[16,64,8,128]{3,1,2,0:T(8,128)(2,1)S(1)}, u32[]{:S(2)}, u32[]{:S(2)}) %all-to-all-start.8) | async-done | bytes 2097184 | tf_op jit(solution)/shard_map/all_to_all | solution.py:56
  475.6 11.4 %all-to-all-start.9 = ((bf16[16,64,8,128]{3,1,2,0:T(8,128)(2,1)}), bf16[16,64,8,128]{3,1,2,0:T(8,128)(2,1)S(1)}, u32[]{:S(2)}, u32[]{:S(2)}) async-start(bf16[16,64,8,128]{3,1,2,0:T(8,128)(2,1)} %bitcast.213), calls=%async_computation.9 | async-start | bytes 4194304 | tf_op jit(solution)/shard_map/all_to_all | solution.py:56
  498.4 7.9 %fusion.18 = f32[4,256,1024]{2,1,0:T(8,128)} fusion(bf16[2,8,1024,1024]{3,2,1,0:T(8,128)(2,1)} %param.15, bf16[4,1024,128]{1,2,0:T(8,128)(2,1)S(1)} %get-tuple-element.98, bf16[4,1024,128]{1,2,0:T(8,128)(2,1)S(1)} %get-tuple-element.97), kind=kOutput, calls=%fused_computation.22 | convolution fusion | flops 2151677952 | bytes 14680064 | tf_op jit(solution)/shard_map/hvi,hig->hvg/dot_general | solution.py:90
  506.2 9.1 %multiply_reduce_fusion.4 = f32[]{:T(128)} fusion(f32[4,1024,256]{1,2,0:T(8,128)} %get-tuple-element.122, f32[]{:T(128)S(6)} %mul.331, f32[]{:T(128)S(6)} %div.44, f32[4,256,1024]{2,1,0:T(8,128)} %fusion.18, bf16[4,1024,256]{1,2,0:T(8,128)(2,1)S(1)} %bitcast.238, bf16[2,8,1024,1024]{3,2,1,0:T(8,128)(2,1)} %param.15), kind=kOutput, calls=%fused_computation.71 | convolution fusion | flops 2153775104 | bytes 18874380 | tf_op jit(solution)/shard_map/hvi,hig->hvg/dot_general | solution.py:89
  515.4 12.6 %all-to-all-done.9 = bf16[16,64,8,128]{3,1,2,0:T(8,128)(2,1)S(1)} async-done(((bf16[16,64,8,128]{3,1,2,0:T(8,128)(2,1)}), bf16[16,64,8,128]{3,1,2,0:T(8,128)(2,1)S(1)}, u32[]{:S(2)}, u32[]{:S(2)}) %all-to-all-start.9) | async-done | bytes 2097184 | tf_op jit(solution)/shard_map/all_to_all | solution.py:56
  546.2 11.5 %all-to-all-start.10 = ((f32[16,1,128]{2,1,0:T(1,128)}), f32[16,1,128]{2,1,0:T(1,128)S(1)}, u32[]{:S(2)}, u32[]{:S(2)}) async-start(f32[16,1,128]{2,1,0:T(1,128)} %broadcast_in_dim.14), calls=%async_computation.10 | async-start | bytes 16384 | tf_op jit(solution)/shard_map/all_to_all | solution.py:32
  557.7 11.9 %bitcast_select_fusion.1 = (f32[256,64,128]{0,2,1:T(8,128)}, f32[256,64,128]{0,2,1:T(8,128)}) fusion(f32[64,128,256]{2,1,0:T(8,128)} %get-tuple-element.121, s32[64,128]{1,0:T(8,128)S(1)} %copy-done.10, f32[]{:T(128)S(6)} %mul.325, f32[]{:T(128)S(6)} %div.43, f32[64,128,256]{2,1,0:T(8,128)} %get-tuple-element.124), kind=kLoop, calls=%fused_computation.3 | loop fusion | flops 12582912 | bytes 33587208 | tf_op jit(solution)/shard_map/mul | solution.py:74
  570.1 11.6 %multiply_add_fusion = f32[256,64,128]{0,2,1:T(8,128)} fusion(f32[256,64,128]{0,2,1:T(8,128)} %get-tuple-element.86, f32[256,64,128]{0,2,1:T(8,128)} %get-tuple-element.85, f32[]{:T(128)S(6)} %mul.349, f32[]{:T(128)S(6)} %add.135), kind=kLoop, calls=%fused_computation.38 | loop fusion | flops 6291456 | bytes 25165832 | tf_op jit(solution)/shard_map/add | solution.py:149
  581.7 8.7 %copy.241 = f32[256,64,128]{2,1,0:T(8,128)} copy(f32[256,64,128]{0,2,1:T(8,128)} %multiply_add_fusion) | data formatting | bytes 16777216 | tf_op jit(solution)/shard_map/add | solution.py:149
  (102 shorter events, 181.9 us)
Async XLA Ops:
  8.9 5.6 copy-start.2
  35.1 48.5 %all-to-all-start = ((bf16[16,64,8,128]{3,1,2,0:T(8,128)(2,1)}), bf16[16,64,8,128]{3,1,2,0:T(8,128)(2,1)}, u32[]{:S(2)}, u32[]{:S(2)}) async-start(bf16[16,64,8,128]{3,1,2,0:T(8,128)(2,1)} %bitcast.7), calls=%async_computation | async-start | bytes 4194304 | tf_op jit(solution)/shard_map/all_to_all | solution.py:56
  83.6 52.5 %all-to-all-start.1 = ((bf16[16,64,8,128]{3,1,2,0:T(8,128)(2,1)}), bf16[16,64,8,128]{3,1,2,0:T(8,128)(2,1)}, u32[]{:S(2)}, u32[]{:S(2)}) async-start(bf16[16,64,8,128]{3,1,2,0:T(8,128)(2,1)} %bitcast.228), calls=%async_computation.1 | async-start | bytes 4194304 | tf_op jit(solution)/shard_map/all_to_all | solution.py:56
  102.7 33.4 %copy-start.10 = (s32[64,128]{1,0:T(8,128)S(1)}, s32[64,128]{1,0:T(8,128)}, u32[]{:S(2)}) copy-start(s32[64,128]{1,0:T(8,128)} %param.17) | copy-start | bytes 98308
  145.7 18.3 %all-to-all-start.2 = ((f32[16,1,128]{2,1,0:T(1,128)}), f32[16,1,128]{2,1,0:T(1,128)S(1)}, u32[]{:S(2)}, u32[]{:S(2)}) async-start(f32[16,1,128]{2,1,0:T(1,128)} %broadcast_in_dim.12), calls=%async_computation.2 | async-start | bytes 16384 | tf_op jit(solution)/shard_map/all_to_all | solution.py:32
  164.0 47.1 %all-to-all-start.3 = ((bf16[16,64,8,128]{3,1,2,0:T(8,128)(2,1)}), bf16[16,64,8,128]{3,1,2,0:T(8,128)(2,1)}, u32[]{:S(2)}, u32[]{:S(2)}) async-start(bf16[16,64,8,128]{3,1,2,0:T(8,128)(2,1)} %bitcast.229), calls=%async_computation.3 | async-start | bytes 4194304 | tf_op jit(solution)/shard_map/all_to_all | solution.py:56
  211.1 65.0 %all-to-all-start.4 = ((bf16[16,64,8,128]{3,1,2,0:T(8,128)(2,1)}), bf16[16,64,8,128]{3,1,2,0:T(8,128)(2,1)}, u32[]{:S(2)}, u32[]{:S(2)}) async-start(bf16[16,64,8,128]{3,1,2,0:T(8,128)(2,1)} %bitcast.226), calls=%async_computation.4 | async-start | bytes 4194304 | tf_op jit(solution)/shard_map/all_to_all | solution.py:56
  231.6 7.9 %copy-start.3 = (f32[1,4,1024,128]{2,3,1,0:T(8,128)S(1)}, f32[1,4,1024,128]{2,3,1,0:T(8,128)}, u32[]{:S(2)}) copy-start(f32[1,4,1024,128]{2,3,1,0:T(8,128)} %copy-done.2) | copy-start | bytes 6291460
  231.6 7.9 %copy-start.4 = (f32[1,4,1024,128]{2,3,1,0:T(8,128)S(1)}, f32[1,4,1024,128]{2,3,1,0:T(8,128)}, u32[]{:S(2)}) copy-start(f32[1,4,1024,128]{2,3,1,0:T(8,128)} %copy.263) | copy-start | bytes 6291460
  231.6 7.9 %copy-start.7 = (bf16[4,1024,2,128]{1,3,2,0:T(8,128)(2,1)S(1)}, bf16[4,1024,2,128]{1,3,2,0:T(8,128)(2,1)}, u32[]{:S(2)}) copy-start(bf16[4,1024,2,128]{1,3,2,0:T(8,128)(2,1)} %copy.218) | copy-start | bytes 6291460
  252.4 4.9 copy-start.9
  285.9 47.3 %all-to-all-start.5 = ((bf16[16,64,8,128]{3,1,2,0:T(8,128)(2,1)}), bf16[16,64,8,128]{3,1,2,0:T(8,128)(2,1)}, u32[]{:S(2)}, u32[]{:S(2)}) async-start(bf16[16,64,8,128]{3,1,2,0:T(8,128)(2,1)} %bitcast.227), calls=%async_computation.5 | async-start | bytes 4194304 | tf_op jit(solution)/shard_map/all_to_all | solution.py:56
  292.2 8.2 %copy-start.1 = (f32[1,4,1024,128]{2,3,1,0:T(8,128)S(1)}, f32[1,4,1024,128]{2,3,1,0:T(8,128)}, u32[]{:S(2)}) copy-start(f32[1,4,1024,128]{2,3,1,0:T(8,128)} %copy.265) | copy-start | bytes 6291460
  292.3 8.2 %copy-start.6 = (bf16[4,1024,2,128]{1,3,2,0:T(8,128)(2,1)S(1)}, bf16[4,1024,2,128]{1,3,2,0:T(8,128)(2,1)}, u32[]{:S(2)}) copy-start(bf16[4,1024,2,128]{1,3,2,0:T(8,128)(2,1)} %copy.224) | copy-start | bytes 6291460
  333.2 52.4 %all-to-all-start.6 = ((bf16[16,64,8,128]{3,1,2,0:T(8,128)(2,1)}), bf16[16,64,8,128]{3,1,2,0:T(8,128)(2,1)S(1)}, u32[]{:S(2)}, u32[]{:S(2)}) async-start(bf16[16,64,8,128]{3,1,2,0:T(8,128)(2,1)} %bitcast.50), calls=%async_computation.6 | async-start | bytes 4194304 | tf_op jit(solution)/shard_map/all_to_all | solution.py:56
  425.4 4.2 copy-start
  429.6 44.6 %all-to-all-start.8 = ((bf16[16,64,8,128]{3,1,2,0:T(8,128)(2,1)}), bf16[16,64,8,128]{3,1,2,0:T(8,128)(2,1)S(1)}, u32[]{:S(2)}, u32[]{:S(2)}) async-start(bf16[16,64,8,128]{3,1,2,0:T(8,128)(2,1)} %bitcast.236), calls=%async_computation.8 | async-start | bytes 4194304 | tf_op jit(solution)/shard_map/all_to_all | solution.py:56
  474.2 1.3 copy-start.5
  475.6 52.4 %all-to-all-start.9 = ((bf16[16,64,8,128]{3,1,2,0:T(8,128)(2,1)}), bf16[16,64,8,128]{3,1,2,0:T(8,128)(2,1)S(1)}, u32[]{:S(2)}, u32[]{:S(2)}) async-start(bf16[16,64,8,128]{3,1,2,0:T(8,128)(2,1)} %bitcast.213), calls=%async_computation.9 | async-start | bytes 4194304 | tf_op jit(solution)/shard_map/all_to_all | solution.py:56
  498.3 7.9 %copy-start.8 = (bf16[4,1024,2,128]{1,3,2,0:T(8,128)(2,1)S(1)}, bf16[4,1024,2,128]{1,3,2,0:T(8,128)(2,1)}, u32[]{:S(2)}) copy-start(bf16[4,1024,2,128]{1,3,2,0:T(8,128)(2,1)} %copy.235) | copy-start | bytes 6291460
  532.7 5.0 copy-start.11
  546.2 23.7 %all-to-all-start.10 = ((f32[16,1,128]{2,1,0:T(1,128)}), f32[16,1,128]{2,1,0:T(1,128)S(1)}, u32[]{:S(2)}, u32[]{:S(2)}) async-start(f32[16,1,128]{2,1,0:T(1,128)} %broadcast_in_dim.14), calls=%async_computation.10 | async-start | bytes 16384 | tf_op jit(solution)/shard_map/all_to_all | solution.py:32
where the time goes:
time: 601 us; the launch traced here: 591 us
  matrix products  166 us (28%)
  waiting for transfers between devices  148 us (25%)
  local copies, waits for them, and re-layouts  109 us (18%)
  starting transfers between devices  92.3 us (15%)
  other arithmetic  49.5 us (8%)
  blocking collectives  17.4 us (3%)
  between operations  8.58 us (1%)
    all_to_all x8, waiting for transfers between devices, exchange(): lax.all_to_all(block, 'freq', split_axis=0, concat_axis=0, tiled=True)  148 us
    all_to_all x8, starting transfers between devices, exchange(): lax.all_to_all(block, 'freq', split_axis=0, concat_axis=0, tiled=True)  69.6 us
    dot_general x4, matrix products, forward_part(): jnp.einsum('hvi,hig->hvg', real[c], spec, preferred_element_type=jnp.floa...  37.5 us
    dot_general x4, matrix products, to_time(): jnp.einsum('kt,rkq->rtq', tables[c], block, preferred_element_type=jnp.fl...  36.9 us
    dot_general x4, matrix products, image_part(): jnp.einsum('hvi,hvg->hig', real[c], low, preferred_element_type=jnp.float32)  29.2 us
    dot_general x4, matrix products, forward_part(): jnp.einsum('hvi,hig->hvg', imag[c], turned, preferred_element_type=jnp.fl...  28.9 us
    all_to_all x2, starting transfers between devices, joint(): lax.all_to_all(spread, 'freq', split_axis=0, concat_axis=0, tiled=True)  22.7 us
    dot_general x4, matrix products, image_part(): jnp.einsum('hvi,hvg->hig', imag[c], turned, preferred_element_type=jnp.fl...  19.2 us
  transfers between devices with their start and end apart: 10, of which 7 were waited for; matrix products, arithmetic and copies ran while one was open for 35% of the time, Pallas kernels for 0%

commit v1 on v0

v1 whole, which is shorter than its diff:
```python
import functools
import math

import jax
import jax.numpy as jnp
import numpy as np
from jax import lax
from jax.experimental import pallas as pl
from jax.experimental.pallas import tpu as pltpu
from jax.sharding import PartitionSpec as P

MESH = pl.DeviceIdType.MESH
ROW = 16
F32 = jnp.float32
BF16 = jnp.bfloat16


def dft_table(bins_total):
    samples = np.arange(2 * bins_total)
    bins = np.arange(bins_total)
    phase = (bins[:, None] * samples[None, :] % (2 * bins_total)) * (math.pi / bins_total)
    factor = 1.0 / math.sqrt(bins_total)
    both = np.stack([np.cos(phase) * factor, -np.sin(phase) * factor], axis=1)
    return both.reshape(2 * bins_total, 2 * bins_total).astype(np.float32)


def swap_matrix():
    size = ROW * ROW
    matrix = np.zeros((size, size), np.float32)
    for a in range(ROW):
        for b in range(ROW):
            matrix[b * ROW + a, a * ROW + b] = 1.0
    return matrix


def fold(values):
    rows, lanes = values.shape
    return jnp.sum(values.reshape(rows // 8, 8, lanes), axis=0)


def total(part):
    return jnp.sum(jnp.sum(part, axis=0, keepdims=True), axis=1, keepdims=True)


def dot(a, b):
    return jnp.dot(a, b, preferred_element_type=F32)


def body(members, kern_hbm, rec_hbm, onset_ref, to_time_ref, to_freq_ref, swap_ref,
         first_hbm, second_hbm, resid_hbm, coef_ref,
         kern, fbuf, rbuf, sbuf, abuf, field, slot, turned, mid, sums,
         kern_sem, slot_sem, out_sem, field_sem, send_sem, recv_sem, sum_send, sum_recv):
    me = lax.axis_index("freq")
    bins2, receivers, focal = fbuf.shape
    bins = bins2 // 2
    rows_k, rec_local, _ = rbuf.shape
    sources = kern.shape[2]
    blocks = rec_local // ROW
    times = field.shape[1] // ROW
    others = members - 1
    tile_v = min(256, sources)
    tile_i = min(256, receivers)
    group_k = min(4, rows_k // ROW)
    group_r = 4

    def peer(j):
        step = 1 + lax.rem(j + members // 2 - 1, others)
        return lax.rem(me + step, members)

    def kern_copy(f):
        return pltpu.make_async_copy(kern_hbm.at[:, f], kern.at[:, f], kern_sem.at[f])

    def rec_copy(f):
        s = lax.rem(f, 2)
        return pltpu.make_async_copy(rec_hbm.at[:, f], slot.at[s], slot_sem.at[s])

    def resid_in(f):
        s = lax.rem(f, 2)
        return pltpu.make_async_copy(resid_hbm.at[f], slot.at[s], slot_sem.at[s])

    def resid_out(f):
        s = lax.rem(f, 2)
        return pltpu.make_async_copy(slot.at[s], resid_hbm.at[f], out_sem.at[s])

    def field_copy(ib, out):
        return pltpu.make_async_copy(field.at[ib], out.at[ib], field_sem.at[ib])

    def wait_bytes(view, sem):
        pltpu.make_async_copy(view, view, sem).wait()

    def freq_view():
        return fbuf.at[:, pl.ds(0, others * rec_local), :]

    def rec_view():
        return rbuf.at[pl.ds(0, others * bins2), :, :]

    rec_copy(0).start()

    @pl.loop(0, bins)
    def _(f):
        kern_copy(f).start()

    barrier = pltpu.get_barrier_semaphore()

    @pl.loop(0, others)
    def _(j):
        pl.semaphore_signal(barrier, inc=1, device_id={"freq": peer(j)}, device_id_type=MESH)

    pl.semaphore_wait(barrier, others)

    def share(turn, parts):
        for place, part in enumerate(parts):
            sums[turn, me, place] = part

        @pl.loop(0, others)
        def _(j):
            pltpu.make_async_remote_copy(
                src_ref=sums.at[turn, me], dst_ref=sums.at[turn, me],
                send_sem=sum_send.at[turn], recv_sem=sum_recv.at[turn],
                device_id={"freq": peer(j)}, device_id_type=MESH,
            ).start()

    def collect(turn, count):
        wait_bytes(sums.at[turn, pl.ds(0, others)], sum_recv.at[turn])
        wait_bytes(sums.at[turn, pl.ds(0, others)], sum_send.at[turn])
        return [total(jnp.sum(sums[turn, :, place], axis=0)) for place in range(count)]

    def send_images(turn, f):
        @pl.loop(0, others)
        def _(j):
            to = peer(j)
            pltpu.make_async_remote_copy(
                src_ref=fbuf.at[pl.ds(2 * f, 2), pl.ds(pl.multiple_of(to * rec_local, ROW), rec_local), :],
                dst_ref=rbuf.at[pl.ds(me * bins2 + 2 * f, 2), :, :],
                send_sem=send_sem.at[turn], recv_sem=recv_sem.at[turn],
                device_id={"freq": to}, device_id_type=MESH,
            ).start()

    def send_spectra(turn, ib):
        start = pl.multiple_of(me * rec_local + ib * ROW, ROW)

        @pl.loop(0, others)
        def _(j):
            to = peer(j)
            pltpu.make_async_remote_copy(
                src_ref=sbuf.at[pl.ds(to * bins2, bins2), pl.ds(pl.multiple_of(ib * ROW, ROW), ROW), :],
                dst_ref=abuf.at[:, pl.ds(start, ROW), :],
                send_sem=send_sem.at[turn], recv_sem=recv_sem.at[turn],
                device_id={"freq": to}, device_id_type=MESH,
            ).start()

    def turn_over(v, real, imag):
        both = jnp.concatenate([real, imag], axis=1)
        turned[:, pl.ds(v * tile_v, tile_v)] = both.T.astype(BF16)

    def images(f):
        plain = turned[...]
        cross = jnp.concatenate([plain[focal:], -plain[:focal]], axis=0)
        for i in range(receivers // tile_i):
            cols = pl.ds(i * tile_i, tile_i)
            z = dot(plain, kern[0, f, :, cols]) + dot(cross, kern[1, f, :, cols])
            z = z.T.astype(BF16)
            fbuf[2 * f, cols, :] = z[:, :focal]
            fbuf[2 * f + 1, cols, :] = z[:, focal:]
        mine = pl.ds(pl.multiple_of(me * rec_local, ROW), rec_local)
        rbuf[pl.ds(me * bins2 + 2 * f, 2), :, :] = fbuf[pl.ds(2 * f, 2), mine, :]

    def forward(f, finish, carry):
        real, imag = abuf[2 * f], abuf[2 * f + 1]
        plain = jnp.concatenate([real, imag], axis=1)
        cross = jnp.concatenate([-imag, real], axis=1)
        for v in range(sources // tile_v):
            rows = pl.ds(v * tile_v, tile_v)
            y = dot(kern[0, f, rows, :], plain) + dot(kern[1, f, rows, :], cross)
            carry = finish(v, rows, y[:, :focal], y[:, focal:], carry)
        return carry

    def receivers_side(turn, ib, make_field, carry):
        here = pl.ds(pl.multiple_of(ib * ROW, ROW), ROW)

        @pl.loop(0, rows_k // (ROW * group_k))
        def _(g):
            pieces = []
            for n in range(group_k):
                at = pl.ds((g * group_k + n) * ROW, ROW)
                pieces.append(rbuf[at, here, :].reshape(ROW * ROW, focal))
            out = dot(swap_ref[...], jnp.concatenate(pieces, axis=1)).astype(BF16)
            for n in range(group_k):
                at = pl.ds(pl.multiple_of((g * group_k + n) * ROW, ROW), ROW)
                mid[:, at, :] = out[:, n * focal:(n + 1) * focal].reshape(ROW, ROW, focal)

        steps = lax.broadcasted_iota(jnp.int32, (times, focal), 0)

        def group(g, carry):
            stack = jnp.concatenate([mid[g * group_r + n] for n in range(group_r)], axis=1)
            raw = dot(to_time_ref[...], stack)
            lows = []
            for n in range(group_r):
                r = g * group_r + n
                onset = onset_ref[pl.ds(ib * ROW + r, 1), :]
                kept = jnp.where(steps < onset, raw[:, n * focal:(n + 1) * focal], 0.0)
                kept = make_field(ib, r, kept)
                carry = carry + fold(kept * kept)
                field[ib, pl.ds(r, times, stride=ROW), :] = kept
                lows.append(kept.astype(BF16))
            spec = dot(to_freq_ref[...], jnp.concatenate(lows, axis=1)).astype(BF16)
            for n in range(group_r):
                mid[g * group_r + n] = spec[:, n * focal:(n + 1) * focal]
            return carry

        carry = lax.fori_loop(0, ROW // group_r, group, carry)

        @pl.loop(0, rows_k // (ROW * group_k))
        def _(g):
            pieces = []
            for n in range(group_k):
                at = pl.ds(pl.multiple_of((g * group_k + n) * ROW, ROW), ROW)
                pieces.append(mid[:, at, :].reshape(ROW * ROW, focal))
            out = dot(swap_ref[...], jnp.concatenate(pieces, axis=1)).astype(BF16)
            for n in range(group_k):
                at = pl.ds((g * group_k + n) * ROW, ROW)
                sbuf[at, here, :] = out[:, n * focal:(n + 1) * focal].reshape(ROW, ROW, focal)

        send_spectra(turn, ib)
        start = pl.multiple_of(me * rec_local + ib * ROW, ROW)
        abuf[:, pl.ds(start, ROW), :] = sbuf[pl.ds(me * bins2, bins2), here, :]
        return carry

    zero = jnp.zeros((8, focal), F32)

    def start_step(f, carry):
        @pl.when(f + 1 < bins)
        def _():
            rec_copy(f + 1).start()

        rec_copy(f).wait()
        kern_copy(f).wait()
        s = lax.rem(f, 2)
        for v in range(sources // tile_v):
            rows = pl.ds(v * tile_v, tile_v)
            real, imag = slot[s, 0, rows, :], slot[s, 1, rows, :]
            carry = carry + fold(real * real) + fold(imag * imag)
            turn_over(v, real, imag)
        images(f)
        send_images(0, f)
        return carry

    sum_b = lax.fori_loop(0, bins, start_step, zero)
    rec_copy(0).start()
    wait_bytes(rec_view(), recv_sem.at[0])

    def first_block(ib, carry):
        carry = receivers_side(1, ib, lambda ib, r, kept: kept, carry)
        field_copy(ib, first_hbm).start()
        return carry

    sum_z = lax.fori_loop(0, blocks, first_block, zero)
    share(0, [sum_b, sum_z])
    wait_bytes(freq_view(), send_sem.at[0])
    square_b, square_z = collect(0, 2)
    beta = jnp.sqrt(square_b)
    image_norm = jnp.sqrt(square_z)
    alpha = image_norm / beta
    scale = 1.0 / image_norm
    weight = alpha / beta

    wait_bytes(freq_view(), recv_sem.at[1])
    wait_bytes(rec_view(), send_sem.at[1])

    def middle_step(f, carry):
        @pl.when(f >= 1)
        def _():
            resid_out(f - 1).wait()

        @pl.when(f + 1 < bins)
        def _():
            rec_copy(f + 1).start()

        rec_copy(f).wait()
        s = lax.rem(f, 2)

        def finish(v, rows, real, imag, carry):
            real = real * scale - weight * slot[s, 0, rows, :]
            imag = imag * scale - weight * slot[s, 1, rows, :]
            slot[s, 0, rows, :] = real
            slot[s, 1, rows, :] = imag
            turn_over(v, real, imag)
            return carry + fold(real * real) + fold(imag * imag)

        carry = forward(f, finish, carry)
        resid_out(f).start()
        images(f)
        send_images(2, f)
        return carry

    sum_u = lax.fori_loop(0, bins, middle_step, zero)
    share(1, [sum_u])
    resid_out(bins - 1).wait()
    resid_in(0).start()
    (square_u,) = collect(1, 1)
    beta_u = jnp.sqrt(square_u)
    data_scale = 1.0 / beta_u
    back = beta_u * scale

    wait_bytes(rec_view(), recv_sem.at[2])
    wait_bytes(freq_view(), send_sem.at[2])

    def second_block(ib, carry):
        field_copy(ib, first_hbm).wait()

        def make_field(ib, r, kept):
            return kept * data_scale - back * field[ib, pl.ds(r, times, stride=ROW), :]

        carry = receivers_side(3, ib, make_field, carry)
        field_copy(ib, second_hbm).start()
        return carry

    sum_v = lax.fori_loop(0, blocks, second_block, zero)
    share(2, [sum_v])
    (square_v,) = collect(2, 1)
    alpha_v = jnp.sqrt(square_v)
    last_scale = 1.0 / alpha_v
    last_weight = alpha_v * data_scale

    wait_bytes(freq_view(), recv_sem.at[3])
    wait_bytes(rec_view(), send_sem.at[3])

    def last_step(f, carry):
        @pl.when(f + 1 < bins)
        def _():
            resid_in(f + 1).start()

        resid_in(f).wait()
        s = lax.rem(f, 2)

        def finish(v, rows, real, imag, carry):
            real = real * last_scale - last_weight * slot[s, 0, rows, :]
            imag = imag * last_scale - last_weight * slot[s, 1, rows, :]
            return carry + fold(real * real) + fold(imag * imag)

        return forward(f, finish, carry)

    sum_last = lax.fori_loop(0, bins, last_step, zero)
    share(3, [sum_last])

    @pl.loop(0, blocks)
    def _(ib):
        field_copy(ib, second_hbm).wait()

    (square_last,) = collect(3, 1)

    rho = jnp.sqrt(alpha * alpha + square_u)
    cosine, sine = alpha / rho, beta_u / rho
    phi = cosine * beta
    phibar = sine * beta
    theta = sine * alpha_v
    rhobar = -cosine * alpha_v
    rho_last = jnp.sqrt(rhobar * rhobar + square_last)
    step_last = rhobar / rho_last * phibar / rho_last
    on_first = (phi / rho - step_last * theta / rho) * scale
    on_second = step_last * last_scale
    coef_ref[0] = jnp.broadcast_to(on_first, (8, focal))
    coef_ref[1] = jnp.broadcast_to(on_second, (8, focal))


def make_step(mesh):
    members = mesh.shape["freq"]

    def step(kernel, recorded, onset_time):
        _, bins, sources, receivers = kernel.shape
        rec_local, focal = onset_time.shape
        times = 2 * bins * members
        blocks = rec_local // ROW
        table = dft_table(bins * members)
        any_space = pl.BlockSpec(memory_space=pl.ANY)
        vmem = pl.BlockSpec(memory_space=pltpu.VMEM)
        shape = jax.ShapeDtypeStruct
        first, second, _, coef = pl.pallas_call(
            functools.partial(body, members),
            out_shape=(
                shape((blocks, times * ROW, focal), F32),
                shape((blocks, times * ROW, focal), F32),
                shape((bins, 2, sources, focal), F32),
                shape((2, 8, focal), F32),
            ),
            in_specs=[any_space, any_space, vmem, vmem, vmem, vmem],
            out_specs=(any_space, any_space, any_space, vmem),
            scratch_shapes=[
                pltpu.VMEM((2, bins, sources, receivers), BF16),
                pltpu.VMEM((2 * bins, receivers, focal), BF16),
                pltpu.VMEM((times, rec_local, focal), BF16),
                pltpu.VMEM((times, rec_local, focal), BF16),
                pltpu.VMEM((2 * bins, receivers, focal), BF16),
                pltpu.VMEM((blocks, times * ROW, focal), F32),
                pltpu.VMEM((2, 2, sources, focal), F32),
                pltpu.VMEM((2 * focal, sources), BF16),
                pltpu.VMEM((ROW, times, focal), BF16),
                pltpu.VMEM((4, members, 2, 8, focal), F32),
                pltpu.SemaphoreType.DMA((bins,)),
                pltpu.SemaphoreType.DMA((2,)),
                pltpu.SemaphoreType.DMA((2,)),
                pltpu.SemaphoreType.DMA((blocks,)),
                pltpu.SemaphoreType.DMA((4,)),
                pltpu.SemaphoreType.DMA((4,)),
                pltpu.SemaphoreType.DMA((4,)),
                pltpu.SemaphoreType.DMA((4,)),
            ],
            compiler_params=pltpu.CompilerParams(
                collective_id=0, has_side_effects=True, vmem_limit_bytes=67043328
            ),
            name="lsqr",
        )(
            kernel, recorded, onset_time,
            jnp.asarray(table.T, BF16), jnp.asarray(table, BF16), jnp.asarray(swap_matrix(), BF16),
        )
        both = coef[0, 0, 0] * first + coef[1, 0, 0] * second
        both = both.reshape(blocks, times, ROW, focal).transpose(1, 0, 2, 3)
        return both.reshape(times, rec_local, focal)

    return step


def solution(mesh):
    placed = (
        P(None, ("grp", "freq"), None, None),
        P(None, ("grp", "freq"), None, None),
        P(("grp", "freq"), None),
    )
    return jax.shard_map(
        make_step(mesh), mesh=mesh, in_specs=placed, out_specs=P(None, ("grp", "freq"), None), check_vma=False
    )
```

time: 601 us -> 432 us (0.72); the launches traced: 591 us -> 432 us
  Pallas kernels: 0 us -> 412 us
  matrix products: 166 us -> 0 us
  waiting for transfers between devices: 148 us -> 0 us
  local copies, waits for them, and re-layouts: 109 us -> 9.31 us
  starting transfers between devices: 92.3 us -> 0 us
  other arithmetic: 49.5 us -> 11.1 us
  blocking collectives: 17.4 us -> 0 us
  between operations: 8.58 us -> 0.01 us
    pallas_call x0 -> x1, Pallas kernels: none -> 412 us  [step(): pl.pallas_call(functools.partial(body, members), out_shape=(shape((blocks...]
    dot_general x24 -> x0, matrix products: 166 us -> none  [the longest x4 37.5 us: forward_part(): jnp.einsum('hvi,hig->hvg', real[c], spec, preferred_element_type=jnp.floa...]
    all_to_all x10 -> x0, waiting for transfers between devices: 148 us -> none  [the longest x8 148 us: exchange(): lax.all_to_all(block, 'freq', split_axis=0, concat_axis=0, tiled=True)]
    all_to_all x10 -> x0, starting transfers between devices: 92.3 us -> none  [the longest x8 69.6 us: exchange(): lax.all_to_all(block, 'freq', split_axis=0, concat_axis=0, tiled=True)]
    reshape x10 -> x0, local copies, waits for them, and re-layouts: 23 us -> none  [the longest x4 12.2 us: image_part(): z = z.astype(jnp.bfloat16).reshape(part, members, rec_local, 2, focal)]
    transpose x10 -> x1, local copies, waits for them, and re-layouts: 28.9 us -> 8.1 us  [step(): both = both.reshape(blocks, times, ROW, focal).transpose(1, 0, 2, 3)]
    all_to_all x1 -> x0, blocking collectives: 17.4 us -> none  [joint(): lax.all_to_all(spread, 'freq', split_axis=0, concat_axis=0, tiled=True)]
    convert_element_type x4 -> x0, local copies, waits for them, and re-layouts: 13.6 us -> none  [image_part(): z = z.astype(jnp.bfloat16).reshape(part, members, rec_local, 2, focal)]
  transfers between devices with their start and end apart: 10 -> 0, of which waited for: 7 -> 0; matrix products, arithmetic and copies ran while one was open for 35% -> 0% of each run, Pallas kernels for 0% -> 0%
where the time goes in v1:
time: 432 us
  Pallas kernels  412 us (95%)
  other arithmetic  11.1 us (3%)
  local copies, waits for them, and re-layouts  9.31 us (2%)
    pallas_call x1, Pallas kernels, step(): pl.pallas_call(functools.partial(body, members), out_shape=(shape((blocks...  412 us
    add x1, other arithmetic, step(): both = coef[0, 0, 0] * first + coef[1, 0, 0] * second  11.1 us

profile of v1, /device:TPU:0, one launch (start us, length us, event | category | flops | bytes accessed | tf_op | source)
XLA Modules:
  0.0 431.9 jit_solution(1044309128293803529)
XLA Ops:
  0.0 411.6 %lsqr.1 = (f32[4,4096,128]{2,1,0:T(8,128)}, f32[4,4096,128]{2,1,0:T(8,128)}, f32[8,2,1024,128]{3,2,1,0:T(8,128)}, f32[2,8,128]{2,1,0:T(8,128)}) custom-call(bf16[2,8,1024,1024]{3,2,1,0:T(8,128)(2,1)} %kern_hbm.1, f32[2,8,1024,128]{3,2,1,0:T(8,128)} %rec_hbm.1, s32[64,128]{1,0:T(8,128)} %onset_ref.1, bf16[256,256]{1,0:T(8,128)(2,1)} %constant.6.clone.to_time_ref, ...), custom_call_target="tpu_custom_call" | custom-call | tf_op jit(solution)/shard_map/lsqr/pallas_call | solution.py:378
  411.6 1.2 fusion
  412.8 11.1 %multiply_add_fusion = f32[4,4096,128]{2,1,0:T(8,128)} fusion(f32[4,4096,128]{2,1,0:T(8,128)} %get-tuple-element.10, f32[4,4096,128]{2,1,0:T(8,128)} %get-tuple-element.9, f32[]{:T(128)} %bitcast.1, f32[]{:T(128)} %bitcast), kind=kLoop, calls=%fused_computation | loop fusion | flops 6291456 | bytes 25165832 | tf_op jit(solution)/shard_map/add | solution.py:416
  423.9 8.1 %copy.7 = f32[256,4,16,128]{3,2,1,0:T(8,128)} copy(f32[256,4,16,128]{3,2,0,1:T(8,128)} %bitcast.6) | data formatting | bytes 16777216 | tf_op jit(solution)/shard_map/transpose | solution.py:417

commit v2 on v1

v2 whole, which is shorter than its diff:
```python
import functools
import math

import jax
import jax.numpy as jnp
from jax import lax
from jax.experimental import pallas as pl
from jax.experimental.pallas import tpu as pltpu
from jax.sharding import PartitionSpec as P

MESH = pl.DeviceIdType.MESH
ROW = 16
DEPTH = 3
VMEM_MAIN = 36 * 2**20
VMEM_WEIGH = 12 * 2**20
F32 = jnp.float32
BF16 = jnp.bfloat16


def fill_tables(to_time_ref, to_freq_ref, swap_ref):
    times = to_freq_ref.shape[0]
    row = lax.broadcasted_iota(jnp.int32, (times, times), 0)
    sample = lax.broadcasted_iota(jnp.int32, (times, times), 1)
    turn = lax.rem(lax.div(row, 2) * sample + lax.rem(row, 2) * (times // 4), times)
    factor = 1.0 / math.sqrt(times // 2)
    table = jnp.cos(turn.astype(F32) * (2.0 * math.pi / times)) * factor
    to_freq_ref[...] = table.astype(BF16)
    to_time_ref[...] = table.T.astype(BF16)
    size = ROW * ROW
    row = lax.broadcasted_iota(jnp.int32, (size, size), 0)
    column = lax.broadcasted_iota(jnp.int32, (size, size), 1)
    target = lax.rem(row, ROW) * ROW + lax.div(row, ROW)
    swap_ref[...] = jnp.where(column == target, 1.0, 0.0).astype(BF16)


def fold(values):
    rows, lanes = values.shape
    return jnp.sum(values.reshape(rows // 8, 8, lanes), axis=0)


def total(part):
    return jnp.sum(jnp.sum(part, axis=0, keepdims=True), axis=1, keepdims=True)


def dot(a, b):
    return jnp.dot(a, b, preferred_element_type=F32)


def body(members, kern_hbm, rec_hbm, onset_ref,
         first_ref, second_ref, resid_hbm, coef_ref,
         kern, fbuf, rbuf, sbuf, abuf, slot, turned, mid, sums,
         to_time_ref, to_freq_ref, swap_ref,
         kern_sem, slot_sem, out_sem, image_send, image_recv, spec_send, early_recv, last_recv,
         sum_send, sum_recv):
    me = lax.axis_index("freq")
    bins2, receivers, focal = fbuf.shape
    bins = bins2 // 2
    rows_k, rec_local, _ = rbuf.shape
    sources = kern.shape[2]
    blocks = rec_local // ROW
    times = first_ref.shape[1] // ROW
    chunks = 2 if blocks % 2 == 0 else 1
    per_chunk = blocks // chunks
    part = per_chunk * ROW
    others = members - 1
    tile_v = min(256, sources)
    tile_i = min(256, receivers)
    group_k = min(4, rows_k // ROW)
    group_r = 4

    def peer(j):
        step = 1 + lax.rem(j + members // 2 - 1, others)
        return lax.rem(me + step, members)

    def kern_copy(g):
        s = lax.rem(g, DEPTH)
        return pltpu.make_async_copy(kern_hbm.at[:, lax.rem(g, bins)], kern.at[s], kern_sem.at[s])

    def kern_step(g):
        @pl.when(g + DEPTH - 1 < 3 * bins)
        def _():
            kern_copy(g + DEPTH - 1).start()

        kern_copy(g).wait()
        return lax.rem(g, DEPTH)

    def rec_copy(f):
        s = lax.rem(f, 2)
        return pltpu.make_async_copy(rec_hbm.at[:, f], slot.at[s], slot_sem.at[s])

    def resid_in(f):
        s = lax.rem(f, 2)
        return pltpu.make_async_copy(resid_hbm.at[f], slot.at[s], slot_sem.at[s])

    def resid_out(f):
        s = lax.rem(f, 2)
        return pltpu.make_async_copy(slot.at[s], resid_hbm.at[f], out_sem.at[s])

    def wait_bytes(view, sem):
        pltpu.make_async_copy(view, view, sem).wait()

    def image_bytes():
        return rbuf.at[pl.ds(0, others * bins2), pl.ds(0, part), :]

    def spectra_bytes(count, rows):
        return abuf.at[pl.ds(0, count), pl.ds(0, others * rows), :]

    rec_copy(0).start()
    kern_copy(0).start()

    barrier = pltpu.get_barrier_semaphore()

    @pl.loop(0, others)
    def _(j):
        pl.semaphore_signal(barrier, inc=1, device_id={"freq": peer(j)}, device_id_type=MESH)

    def share(turn, parts):
        for place, part in enumerate(parts):
            sums[turn, me, place] = part

        @pl.loop(0, others)
        def _(j):
            pltpu.make_async_remote_copy(
                src_ref=sums.at[turn, me], dst_ref=sums.at[turn, me],
                send_sem=sum_send.at[turn], recv_sem=sum_recv.at[turn],
                device_id={"freq": peer(j)}, device_id_type=MESH,
            ).start()

    def collect(turn, count):
        wait_bytes(sums.at[turn, pl.ds(0, others)], sum_recv.at[turn])
        wait_bytes(sums.at[turn, pl.ds(0, others)], sum_send.at[turn])
        return [total(jnp.sum(sums[turn, :, place], axis=0)) for place in range(count)]

    def send_images(turn, c, first, count):
        @pl.loop(0, others)
        def _(j):
            to = peer(j)
            pltpu.make_async_remote_copy(
                src_ref=fbuf.at[pl.ds(first, count), pl.ds(pl.multiple_of(to * rec_local + c * part, ROW), part), :],
                dst_ref=rbuf.at[pl.ds(me * bins2 + first, count), pl.ds(c * part, part), :],
                send_sem=image_send.at[turn], recv_sem=image_recv.at[turn, c],
                device_id={"freq": to}, device_id_type=MESH,
            ).start()

    def send_spectra(turn, first, count, row, rows, recv):
        @pl.loop(0, others)
        def _(j):
            to = peer(j)
            pltpu.make_async_remote_copy(
                src_ref=sbuf.at[pl.ds(to * bins2 + first, count), pl.ds(pl.multiple_of(row, ROW), rows), :],
                dst_ref=abuf.at[pl.ds(first, count), pl.ds(pl.multiple_of(me * rec_local + row, ROW), rows), :],
                send_sem=spec_send.at[turn], recv_sem=recv,
                device_id={"freq": to}, device_id_type=MESH,
            ).start()

    def send_last(turn):
        @pl.loop(0, bins)
        def _(f):
            send_spectra(turn, 2 * f, 2, (chunks - 1) * part, part, last_recv.at[turn, f])

    def send_rest(turn):
        for c in range(1, chunks):
            send_images(turn, c, 0, bins2)

    def turn_over(v, real, imag):
        both = jnp.concatenate([real, imag], axis=1)
        turned[:, pl.ds(v * tile_v, tile_v)] = both.T.astype(BF16)

    def images(f, k):
        plain = turned[...]
        cross = jnp.concatenate([plain[focal:], -plain[:focal]], axis=0)
        for i in range(receivers // tile_i):
            cols = pl.ds(i * tile_i, tile_i)
            z = dot(plain, kern[k, 0, :, cols]) + dot(cross, kern[k, 1, :, cols])
            z = z.T.astype(BF16)
            fbuf[2 * f, cols, :] = z[:, :focal]
            fbuf[2 * f + 1, cols, :] = z[:, focal:]
        mine = pl.ds(pl.multiple_of(me * rec_local, ROW), rec_local)
        rbuf[pl.ds(me * bins2 + 2 * f, 2), :, :] = fbuf[pl.ds(2 * f, 2), mine, :]

    def forward(f, k, finish, carry):
        real, imag = abuf[2 * f], abuf[2 * f + 1]
        plain = jnp.concatenate([real, imag], axis=1)
        cross = jnp.concatenate([-imag, real], axis=1)
        for v in range(sources // tile_v):
            rows = pl.ds(v * tile_v, tile_v)
            y = dot(kern[k, 0, rows, :], plain) + dot(kern[k, 1, rows, :], cross)
            carry = finish(v, rows, y[:, :focal], y[:, focal:], carry)
        return carry

    def receivers_side(turn, ib, field, make_field, carry):
        here = pl.ds(pl.multiple_of(ib * ROW, ROW), ROW)

        @pl.when(lax.rem(ib, per_chunk) == 0)
        def _():
            wait_bytes(image_bytes(), image_recv.at[turn, lax.div(ib, per_chunk)])

        @pl.loop(0, rows_k // (ROW * group_k))
        def _(g):
            pieces = []
            for n in range(group_k):
                at = pl.ds((g * group_k + n) * ROW, ROW)
                pieces.append(rbuf[at, here, :].reshape(ROW * ROW, focal))
            out = dot(swap_ref[...], jnp.concatenate(pieces, axis=1)).astype(BF16)
            for n in range(group_k):
                at = pl.ds(pl.multiple_of((g * group_k + n) * ROW, ROW), ROW)
                mid[:, at, :] = out[:, n * focal:(n + 1) * focal].reshape(ROW, ROW, focal)

        steps = lax.broadcasted_iota(jnp.int32, (times, focal), 0)

        def group(g, carry):
            stack = jnp.concatenate([mid[g * group_r + n] for n in range(group_r)], axis=1)
            raw = dot(to_time_ref[...], stack)
            lows = []
            for n in range(group_r):
                r = g * group_r + n
                onset = onset_ref[pl.ds(ib * ROW + r, 1), :]
                kept = jnp.where(steps < onset, raw[:, n * focal:(n + 1) * focal], 0.0)
                kept = make_field(ib, r, kept)
                carry = carry + fold(kept * kept)
                field[ib, pl.ds(r, times, stride=ROW), :] = kept
                lows.append(kept.astype(BF16))
            spec = dot(to_freq_ref[...], jnp.concatenate(lows, axis=1)).astype(BF16)
            for n in range(group_r):
                mid[g * group_r + n] = spec[:, n * focal:(n + 1) * focal]
            return carry

        carry = lax.fori_loop(0, ROW // group_r, group, carry)

        @pl.loop(0, rows_k // (ROW * group_k))
        def _(g):
            pieces = []
            for n in range(group_k):
                at = pl.ds(pl.multiple_of((g * group_k + n) * ROW, ROW), ROW)
                pieces.append(mid[:, at, :].reshape(ROW * ROW, focal))
            out = dot(swap_ref[...], jnp.concatenate(pieces, axis=1)).astype(BF16)
            for n in range(group_k):
                at = pl.ds((g * group_k + n) * ROW, ROW)
                sbuf[at, here, :] = out[:, n * focal:(n + 1) * focal].reshape(ROW, ROW, focal)

        if chunks > 1:
            @pl.when(ib < blocks - per_chunk)
            def _():
                send_spectra(turn, 0, bins2, ib * ROW, ROW, early_recv.at[turn])

        start = pl.multiple_of(me * rec_local + ib * ROW, ROW)
        abuf[:, pl.ds(start, ROW), :] = sbuf[pl.ds(me * bins2, bins2), here, :]
        return carry

    zero = jnp.zeros((8, focal), F32)

    def start_step(f, carry):
        @pl.when(f + 1 < bins)
        def _():
            rec_copy(f + 1).start()

        rec_copy(f).wait()

        @pl.when(f == 0)
        def _():
            for g in range(1, DEPTH - 1):
                kern_copy(g).start()

        s = lax.rem(f, 2)
        for v in range(sources // tile_v):
            rows = pl.ds(v * tile_v, tile_v)
            real, imag = slot[s, 0, rows, :], slot[s, 1, rows, :]
            carry = carry + fold(real * real) + fold(imag * imag)
            turn_over(v, real, imag)
        images(f, kern_step(f))

        @pl.when(f == 0)
        def _():
            pl.semaphore_wait(barrier, others)

        send_images(0, 0, 2 * f, 2)
        return carry

    sum_b = lax.fori_loop(0, bins, start_step, zero)
    rec_copy(0).start()
    send_rest(0)
    fill_tables(to_time_ref, to_freq_ref, swap_ref)

    def first_block(ib, carry):
        return receivers_side(0, ib, first_ref, lambda ib, r, kept: kept, carry)

    sum_z = lax.fori_loop(0, blocks, first_block, zero)
    share(0, [sum_b, sum_z])
    send_last(0)
    wait_bytes(fbuf.at[:, pl.ds(0, others * rec_local), :], image_send.at[0])
    square_b, square_z = collect(0, 2)
    beta = jnp.sqrt(square_b)
    image_norm = jnp.sqrt(square_z)
    alpha = image_norm / beta
    scale = 1.0 / image_norm
    weight = alpha / beta

    if chunks > 1:
        wait_bytes(spectra_bytes(bins2, rec_local - part), early_recv.at[0])

    def middle_step(f, carry):
        @pl.when(f >= 1)
        def _():
            resid_out(f - 1).wait()

        @pl.when(f + 1 < bins)
        def _():
            rec_copy(f + 1).start()

        rec_copy(f).wait()
        s = lax.rem(f, 2)

        def finish(v, rows, real, imag, carry):
            real = real * scale - weight * slot[s, 0, rows, :]
            imag = imag * scale - weight * slot[s, 1, rows, :]
            slot[s, 0, rows, :] = real
            slot[s, 1, rows, :] = imag
            turn_over(v, real, imag)
            return carry + fold(real * real) + fold(imag * imag)

        wait_bytes(spectra_bytes(2, part), last_recv.at[0, f])
        k = kern_step(bins + f)
        carry = forward(f, k, finish, carry)
        resid_out(f).start()
        images(f, k)
        send_images(1, 0, 2 * f, 2)
        return carry

    sum_u = lax.fori_loop(0, bins, middle_step, zero)
    share(1, [sum_u])
    send_rest(1)
    resid_out(bins - 1).wait()
    resid_in(0).start()
    (square_u,) = collect(1, 1)
    beta_u = jnp.sqrt(square_u)
    data_scale = 1.0 / beta_u
    back = beta_u * scale

    wait_bytes(sbuf.at[pl.ds(0, others * bins2)], spec_send.at[0])

    def second_block(ib, carry):
        def make_field(ib, r, kept):
            return kept * data_scale - back * first_ref[ib, pl.ds(r, times, stride=ROW), :]

        return receivers_side(1, ib, second_ref, make_field, carry)

    sum_v = lax.fori_loop(0, blocks, second_block, zero)
    share(2, [sum_v])
    send_last(1)
    (square_v,) = collect(2, 1)
    alpha_v = jnp.sqrt(square_v)
    last_scale = 1.0 / alpha_v
    last_weight = alpha_v * data_scale

    if chunks > 1:
        wait_bytes(spectra_bytes(bins2, rec_local - part), early_recv.at[1])

    def last_step(f, carry):
        @pl.when(f + 1 < bins)
        def _():
            resid_in(f + 1).start()

        resid_in(f).wait()
        s = lax.rem(f, 2)

        def finish(v, rows, real, imag, carry):
            real = real * last_scale - last_weight * slot[s, 0, rows, :]
            imag = imag * last_scale - last_weight * slot[s, 1, rows, :]
            return carry + fold(real * real) + fold(imag * imag)

        wait_bytes(spectra_bytes(2, part), last_recv.at[1, f])
        return forward(f, kern_step(2 * bins + f), finish, carry)

    sum_last = lax.fori_loop(0, bins, last_step, zero)
    share(3, [sum_last])

    wait_bytes(fbuf.at[:, pl.ds(0, others * rec_local), :], image_send.at[1])
    wait_bytes(sbuf.at[pl.ds(0, others * bins2)], spec_send.at[1])

    (square_last,) = collect(3, 1)

    rho = jnp.sqrt(alpha * alpha + square_u)
    cosine, sine = alpha / rho, beta_u / rho
    phi = cosine * beta
    phibar = sine * beta
    theta = sine * alpha_v
    rhobar = -cosine * alpha_v
    rho_last = jnp.sqrt(rhobar * rhobar + square_last)
    step_last = rhobar / rho_last * phibar / rho_last
    on_first = (phi / rho - step_last * theta / rho) * scale
    on_second = step_last * last_scale
    coef_ref[0] = jnp.broadcast_to(on_first, (8, focal))
    coef_ref[1] = jnp.broadcast_to(on_second, (8, focal))


def weigh(coef_ref, first_ref, second_ref, out_hbm, held, sem):
    pieces, span = held.shape[0], held.shape[1]
    blocks, _, focal = first_ref.shape
    on_first, on_second = coef_ref[0, 0:1, :], coef_ref[1, 0:1, :]

    def write(n):
        return pltpu.make_async_copy(held.at[n], out_hbm.at[pl.ds(n * span, span)], sem.at[n])

    @pl.loop(0, pieces)
    def _(n):
        rows = pl.ds(pl.multiple_of(n * span * ROW, ROW), span * ROW)
        for ib in range(blocks):
            both = on_first * first_ref[ib, rows, :] + on_second * second_ref[ib, rows, :]
            held[n, :, ib * ROW:(ib + 1) * ROW, :] = both.reshape(span, ROW, focal)
        write(n).start()

    @pl.loop(0, pieces)
    def _(n):
        write(n).wait()


def make_step(mesh):
    members = mesh.shape["freq"]

    def step(kernel, recorded, onset_time):
        _, bins, sources, receivers = kernel.shape
        rec_local, focal = onset_time.shape
        times = 2 * bins * members
        blocks = rec_local // ROW
        hbm = pl.BlockSpec(memory_space=pltpu.HBM)
        vmem = pl.BlockSpec(memory_space=pltpu.VMEM)
        shape = jax.ShapeDtypeStruct
        first, second, _, coef = pl.pallas_call(
            functools.partial(body, members),
            out_shape=(
                shape((blocks, times * ROW, focal), F32),
                shape((blocks, times * ROW, focal), F32),
                shape((bins, 2, sources, focal), F32),
                shape((2, 8, focal), F32),
            ),
            in_specs=[hbm, hbm, vmem],
            out_specs=(vmem, vmem, hbm, vmem),
            scratch_shapes=[
                pltpu.VMEM((DEPTH, 2, sources, receivers), BF16),
                pltpu.VMEM((2 * bins, receivers, focal), BF16),
                pltpu.VMEM((times, rec_local, focal), BF16),
                pltpu.VMEM((times, rec_local, focal), BF16),
                pltpu.VMEM((2 * bins, receivers, focal), BF16),
                pltpu.VMEM((2, 2, sources, focal), F32),
                pltpu.VMEM((2 * focal, sources), BF16),
                pltpu.VMEM((ROW, times, focal), BF16),
                pltpu.VMEM((4, members, 2, 8, focal), F32),
                pltpu.VMEM((times, times), BF16),
                pltpu.VMEM((times, times), BF16),
                pltpu.VMEM((ROW * ROW, ROW * ROW), BF16),
                pltpu.SemaphoreType.DMA((DEPTH,)),
                pltpu.SemaphoreType.DMA((2,)),
                pltpu.SemaphoreType.DMA((2,)),
                pltpu.SemaphoreType.DMA((2,)),
                pltpu.SemaphoreType.DMA((2, 2)),
                pltpu.SemaphoreType.DMA((2,)),
                pltpu.SemaphoreType.DMA((2,)),
                pltpu.SemaphoreType.DMA((2, bins)),
                pltpu.SemaphoreType.DMA((4,)),
                pltpu.SemaphoreType.DMA((4,)),
            ],
            compiler_params=pltpu.CompilerParams(
                collective_id=0, has_side_effects=True, vmem_limit_bytes=VMEM_MAIN
            ),
            name="lsqr",
        )(kernel, recorded, onset_time)
        pieces = 16
        span = times // pieces
        return pl.pallas_call(
            weigh,
            out_shape=shape((times, rec_local, focal), F32),
            in_specs=[vmem, vmem, vmem],
            out_specs=hbm,
            scratch_shapes=[
                pltpu.VMEM((pieces, span, rec_local, focal), F32),
                pltpu.SemaphoreType.DMA((pieces,)),
            ],
            compiler_params=pltpu.CompilerParams(vmem_limit_bytes=VMEM_WEIGH),
            name="weigh",
        )(coef, first, second)

    return step


def solution(mesh):
    placed = (
        P(None, ("grp", "freq"), None, None),
        P(None, ("grp", "freq"), None, None),
        P(("grp", "freq"), None),
    )
    return jax.shard_map(
        make_step(mesh), mesh=mesh, in_specs=placed, out_specs=P(None, ("grp", "freq"), None), check_vma=False
    )
```

time: 432 us -> 389 us (0.900)
  Pallas kernels: 412 us -> 388 us
  other arithmetic: 11.1 us -> 0 us
  local copies, waits for them, and re-layouts: 9.31 us -> 0.76 us
    pallas_call x1, Pallas kernels: 412 us -> 384 us  [step(): pl.pallas_call(functools.partial(body, members), out_shape=(shape((blocks...]
    add x1 -> x0, other arithmetic: 11.1 us -> none  [step(): both = coef[0, 0, 0] * first + coef[1, 0, 0] * second]
    transpose x1 -> x0, local copies, waits for them, and re-layouts: 8.1 us -> none  [step(): both = both.reshape(blocks, times, ROW, focal).transpose(1, 0, 2, 3)]
where the time goes in v2:
time: 389 us; the launch traced here: 388 us
  Pallas kernels  388 us (100%)
    pallas_call x1, Pallas kernels, step(): pl.pallas_call(functools.partial(body, members), out_shape=(shape((blocks...  384 us

profile of v2, /device:TPU:0, one launch (start us, length us, event | category | flops | bytes accessed | tf_op | source)
XLA Modules:
  0.0 388.4 jit_solution(14666382950730436159)
XLA Ops:
  0.0 0.0 copy-start
  0.0 0.8 copy-done
  0.8 384.2 %lsqr.1 = (f32[4,4096,128]{2,1,0:T(8,128)S(1)}, f32[4,4096,128]{2,1,0:T(8,128)S(1)}, f32[8,2,1024,128]{3,2,1,0:T(8,128)}, f32[2,8,128]{2,1,0:T(8,128)S(1)}) custom-call(bf16[2,8,1024,1024]{3,2,1,0:T(8,128)(2,1)} %kern_hbm.1, f32[2,8,1024,128]{3,2,1,0:T(8,128)} %rec_hbm.1, s32[64,128]{1,0:T(8,128)S(1)} %copy-done), custom_call_target="tpu_custom_call" | custom-call | tf_op jit(solution)/shard_map/lsqr/pallas_call | solution.py:428
  385.0 3.5 weigh.1
Async XLA Ops:
  0.0 0.8 copy-start

commit v3 on v2

--- a/solution.py
+++ b/solution.py
@@ -68,9 +68,23 @@
     group_k = min(4, rows_k // ROW)
     group_r = 4
 
-    def peer(j):
-        step = 1 + lax.rem(j + members // 2 - 1, others)
-        return lax.rem(me + step, members)
+    half = members // 2
+    side = lax.div(me, half) * half
+    place = lax.rem(me, half)
+
+    def near_peers(act):
+        @pl.loop(0, half - 1)
+        def _(j):
+            act(side + lax.rem(place + 1 + j, half))
+
+    def far_peers(act):
+        @pl.loop(0, half)
+        def _(j):
+            act(half - side + lax.rem(place + j, half))
+
+    def all_peers(act):
+        near_peers(act)
+        far_peers(act)
 
     def kern_copy(g):
         s = lax.rem(g, DEPTH)
@@ -110,31 +124,36 @@
 
     barrier = pltpu.get_barrier_semaphore()
 
-    @pl.loop(0, others)
-    def _(j):
-        pl.semaphore_signal(barrier, inc=1, device_id={"freq": peer(j)}, device_id_type=MESH)
+    def greet(to):
+        pl.semaphore_signal(barrier, inc=1, device_id={"freq": to}, device_id_type=MESH)
+
+    all_peers(greet)
+
+    lane = lax.broadcasted_iota(jnp.int32, (1, focal), 1)
 
     def share(turn, parts):
-        for place, part in enumerate(parts):
-            sums[turn, me, place] = part
-
-        @pl.loop(0, others)
-        def _(j):
+        row = jnp.broadcast_to(total(parts[0]), (1, focal))
+        for entry, values in enumerate(parts[1:], 1):
+            row = jnp.where(lane < entry, row, total(values))
+        sums[turn, me] = row
+
+        def send(to):
             pltpu.make_async_remote_copy(
                 src_ref=sums.at[turn, me], dst_ref=sums.at[turn, me],
                 send_sem=sum_send.at[turn], recv_sem=sum_recv.at[turn],
-                device_id={"freq": peer(j)}, device_id_type=MESH,
+                device_id={"freq": to}, device_id_type=MESH,
             ).start()
+
+        all_peers(send)
 
     def collect(turn, count):
         wait_bytes(sums.at[turn, pl.ds(0, others)], sum_recv.at[turn])
         wait_bytes(sums.at[turn, pl.ds(0, others)], sum_send.at[turn])
-        return [total(jnp.sum(sums[turn, :, place], axis=0)) for place in range(count)]
+        row = jnp.sum(sums[turn], axis=0)
+        return [jnp.sum(jnp.where(lane == entry, row, 0.0), axis=1, keepdims=True) for entry in range(count)]
 
     def send_images(turn, c, first, count):
-        @pl.loop(0, others)
-        def _(j):
-            to = peer(j)
+        def send(to):
             pltpu.make_async_remote_copy(
                 src_ref=fbuf.at[pl.ds(first, count), pl.ds(pl.multiple_of(to * rec_local + c * part, ROW), part), :],
                 dst_ref=rbuf.at[pl.ds(me * bins2 + first, count), pl.ds(c * part, part), :],
@@ -142,10 +161,10 @@
                 device_id={"freq": to}, device_id_type=MESH,
             ).start()
 
-    def send_spectra(turn, first, count, row, rows, recv):
-        @pl.loop(0, others)
-        def _(j):
-            to = peer(j)
+        all_peers(send)
+
+    def send_spectra(peers, turn, first, count, row, rows, recv):
+        def send(to):
             pltpu.make_async_remote_copy(
                 src_ref=sbuf.at[pl.ds(to * bins2 + first, count), pl.ds(pl.multiple_of(row, ROW), rows), :],
                 dst_ref=abuf.at[pl.ds(first, count), pl.ds(pl.multiple_of(me * rec_local + row, ROW), rows), :],
@@ -153,10 +172,13 @@
                 device_id={"freq": to}, device_id_type=MESH,
             ).start()
 
+        peers(send)
+
     def send_last(turn):
-        @pl.loop(0, bins)
-        def _(f):
-            send_spectra(turn, 2 * f, 2, (chunks - 1) * part, part, last_recv.at[turn, f])
+        for peers in (near_peers, far_peers):
+            @pl.loop(0, bins)
+            def _(f, peers=peers):
+                send_spectra(peers, turn, 2 * f, 2, (chunks - 1) * part, part, last_recv.at[turn, f])
 
     def send_rest(turn):
         for c in range(1, chunks):
@@ -241,7 +263,7 @@
         if chunks > 1:
             @pl.when(ib < blocks - per_chunk)
             def _():
-                send_spectra(turn, 0, bins2, ib * ROW, ROW, early_recv.at[turn])
+                send_spectra(all_peers, turn, 0, bins2, ib * ROW, ROW, early_recv.at[turn])
 
         start = pl.multiple_of(me * rec_local + ib * ROW, ROW)
         abuf[:, pl.ds(start, ROW), :] = sbuf[pl.ds(me * bins2, bins2), here, :]
@@ -444,7 +466,7 @@
                 pltpu.VMEM((2, 2, sources, focal), F32),
                 pltpu.VMEM((2 * focal, sources), BF16),
                 pltpu.VMEM((ROW, times, focal), BF16),
-                pltpu.VMEM((4, members, 2, 8, focal), F32),
+                pltpu.VMEM((4, members, 1, focal), F32),
                 pltpu.VMEM((times, times), BF16),
                 pltpu.VMEM((times, times), BF16),
                 pltpu.VMEM((ROW * ROW, ROW * ROW), BF16),

time: 389 us -> 379 us (0.974)
  Pallas kernels: 388 us -> 378 us
    pallas_call x1, Pallas kernels: 384 us -> 375 us  [step(): pl.pallas_call(functools.partial(body, members), out_shape=(shape((blocks...]
where the time goes in v3:
time: 379 us
  Pallas kernels  378 us (100%)
    pallas_call x1, Pallas kernels, step(): pl.pallas_call(functools.partial(body, members), out_shape=(shape((blocks...  375 us

profile of v3, /device:TPU:0, one launch (start us, length us, event | category | flops | bytes accessed | tf_op | source)
XLA Modules:
  0.0 379.0 jit_solution(6461647574379340681)
XLA Ops:
  0.0 0.0 copy-start
  0.0 0.8 copy-done
  0.8 374.7 %lsqr.1 = (f32[4,4096,128]{2,1,0:T(8,128)S(1)}, f32[4,4096,128]{2,1,0:T(8,128)S(1)}, f32[8,2,1024,128]{3,2,1,0:T(8,128)}, f32[2,8,128]{2,1,0:T(8,128)S(1)}) custom-call(bf16[2,8,1024,1024]{3,2,1,0:T(8,128)(2,1)} %kern_hbm.1, f32[2,8,1024,128]{3,2,1,0:T(8,128)} %rec_hbm.1, s32[64,128]{1,0:T(8,128)S(1)} %copy-done), custom_call_target="tpu_custom_call" | custom-call | tf_op jit(solution)/shard_map/lsqr/pallas_call | solution.py:450
  375.5 3.5 weigh.1
Async XLA Ops:
  0.0 0.8 copy-start
